TPU v7x, 32 devices: a whole 2x2x4 slice. The times are simulated.
32 devices in a mesh: lat: 16 (over z, y, x), lon: 2 (over core).
Axes of the slice: x: 2, y: 2, z: 4, core: 2. Of those that a mesh axis runs over, the one named last changes fastest.
Arguments:
- fields: bfloat16 [2048, 2, 1024], P('lat', 'lon'), may hold values from -6 to 6
- proj_x: bfloat16 [1024, 1024], P('lon'), may hold values from -0.1875 to 0.1875
- proj_z: bfloat16 [1024, 1024], P('lon'), may hold values from -0.1875 to 0.1875
- proj_bc: bfloat16 [1024, 128], P('lon'), may hold values from -0.1875 to 0.1875
- proj_dt: bfloat16 [1024, 16], P('lon'), may hold values from -1 to 1
- conv_x: float32 [4, 1024], replicated, may hold values from -3 to 3
- conv_bc: float32 [4, 128], replicated, may hold values from -3 to 3
- dt_bias: float32 [16], replicated, may hold values from -1 to 0.5
- log_rate: float32 [16], replicated, may hold values from -12 to -2.7
- norm_gain: float32 [1024], replicated, may hold values from 0.1 to 1.9
- proj_out: bfloat16 [1024, 1024], P('lon'), may hold values from -0.1875 to 0.1875
Outputs:
- mixer_out: bfloat16 [2048, 2, 1024], P('lat', 'lon')
All inputs are finite; a program needn't handle non-finite values.
Results may differ from a plain program's by a relative error of at most 0.012.
Values may be sent and summed in bfloat16 or wider, within the bound.
A program may use at most 64 MiB of HBM per device.

v0:
```python
import jax
import jax.numpy as jnp
from jax import lax
from jax.sharding import PartitionSpec as P

norm_epsilon = 1e-05
highest = lax.Precision.HIGHEST


def shifted(block, axis, distance):
    devices = range(lax.axis_size(axis))
    route = [(i - distance, i) for i in devices if i - distance in devices]
    return lax.ppermute(block, axis, route)


def partner_2(block, axis, apart):
    count = lax.axis_size(axis)
    route = []
    for low in range(count):
        high = low | 1 << apart
        if high != low and high < count:
            route += [(low, high), (high, low)]
    return lax.ppermute(block, axis, route)


def causal_conv(values, kernel):
    out_rows = values.shape[0] - kernel.shape[0] + 1
    acc_sum = jnp.zeros((out_rows,) + values.shape[1:], jnp.float32)
    for offset in range(kernel.shape[0]):
        acc_sum = acc_sum + kernel[offset] * values[offset : offset + out_rows]
    return jax.nn.silu(acc_sum).astype(jnp.bfloat16)


def combine(earlier_part, later_part):
    return (
        earlier_part[0] + later_part[0],
        jnp.exp(later_part[0])[..., None] * earlier_part[1] + later_part[1],
    )


def local(
    fields,
    proj_x,
    proj_z,
    proj_bc,
    proj_dt,
    conv_x,
    conv_bc,
    dt_bias,
    log_rate,
    norm_gain,
    proj_out,
):
    band_rows, band_cols, model_width = fields.shape
    margin = conv_x.shape[0] - 1
    head_count = log_rate.shape[0]
    inner_width = proj_x.shape[1]
    state_size = proj_bc.shape[1] // 2
    row_count = fields.shape[0]
    flat_rows = fields.reshape(row_count * band_cols, model_width)
    pieces = (
        lax.all_gather(proj_x, "lon", axis=0, tiled=True),
        lax.all_gather(proj_z, "lon", axis=0, tiled=True),
        lax.all_gather(proj_bc, "lon", axis=0, tiled=True),
        lax.all_gather(proj_dt, "lon", axis=0, tiled=True),
    )
    columns = flat_rows
    projected = tuple(
        (jnp.dot(columns, piece_rows, preferred_element_type=jnp.float32) for piece_rows in pieces)
    )
    inner_pre, gate_pre, bc_pre, dt_pre = [
        result_sum.astype(jnp.bfloat16).reshape(row_count, band_cols, -1)
        for result_sum in projected
    ]
    tail_rows = shifted((inner_pre[band_rows - margin :], bc_pre[band_rows - margin :]), "lat", 1)
    inner_ext = jnp.concatenate([tail_rows[0], inner_pre], 0)
    bc_ext = jnp.concatenate([tail_rows[1], bc_pre], 0)
    inner_act = causal_conv(inner_ext.astype(jnp.float32), conv_x)
    bc_act = causal_conv(bc_ext.astype(jnp.float32), conv_bc)
    step_dt = jax.nn.softplus(dt_pre.astype(jnp.float32) + dt_bias)
    log_step = -jnp.exp(log_rate) * step_dt
    head_inner = inner_act.astype(jnp.float32).reshape(band_rows, band_cols, head_count, -1)
    input_b = bc_act[..., :state_size].astype(jnp.float32)
    read_c = bc_act[..., state_size:].astype(jnp.float32)
    cumulative = jnp.cumsum(log_step, axis=0)
    causal = jnp.arange(band_rows)[:, None] >= jnp.arange(band_rows)[None, :]
    decay_gap = cumulative[:, None] - cumulative[None, :]
    decay = jnp.exp(jnp.where(causal[:, :, None, None], decay_gap, -jnp.inf))
    scores = jnp.einsum("tcn,scn->tsc", read_c, input_b, precision=highest)
    weights = decay * scores[:, :, :, None] * step_dt[None]
    diag_out = jnp.einsum("tsch,schp->tchp", weights, head_inner, precision=highest)
    band_total = cumulative[-1]
    end_weight = jnp.exp(band_total[None] - cumulative) * step_dt
    end_state = jnp.einsum("sch,scn,schp->chnp", end_weight, input_b, head_inner, precision=highest)
    states = end_state.reshape(band_cols, head_count, -1)
    position = lax.axis_index("lat")
    prefix = (jnp.zeros_like(band_total), jnp.zeros_like(states))
    running = (band_total, states)
    for bit_level in range(lax.axis_size("lat").bit_length() - 1):
        partner = partner_2((running[0], running[1]), "lat", bit_level)
        later_half = position // (1 << bit_level) % 2 == 1
        merged_low = combine(partner, running)
        merged_high = combine(running, partner)
        moved_prefix = combine(partner, prefix)
        prefix = (
            jnp.where(later_half, moved_prefix[0], prefix[0]),
            jnp.where(later_half, moved_prefix[1], prefix[1]),
        )
        running = (
            jnp.where(later_half, merged_low[0], merged_high[0]),
            jnp.where(later_half, merged_low[1], merged_high[1]),
        )
    incoming = prefix[1]
    incoming = incoming.reshape(band_cols, head_count, state_size, -1)
    state_out = (
        jnp.einsum("tcn,chnp->tchp", read_c, incoming, precision=highest)
        * jnp.exp(cumulative)[..., None]
    )
    mixed_heads = (diag_out + state_out).reshape(band_rows, band_cols, inner_width)
    gated_out = mixed_heads * jax.nn.silu(gate_pre.astype(jnp.float32))
    normed = (
        gated_out
        * lax.rsqrt(jnp.mean(gated_out * gated_out, -1, keepdims=True) + norm_epsilon)
        * norm_gain
    )
    hidden = normed.astype(jnp.bfloat16).reshape(band_rows * band_cols, inner_width)
    columns = hidden
    result = jnp.dot(
        columns,
        lax.all_gather(proj_out, "lon", axis=0, tiled=True),
        preferred_element_type=jnp.float32,
    )
    return result.astype(jnp.bfloat16).reshape(band_rows, band_cols, model_width)


def solution(mesh):
    return jax.shard_map(
        local,
        mesh=mesh,
        in_specs=(
            P("lat", "lon", None),
            P("lon", None),
            P("lon", None),
            P("lon", None),
            P("lon", None),
            P(),
            P(),
            P(),
            P(),
            P(),
            P("lon", None),
        ),
        out_specs=P("lat", "lon", None),
        check_vma=False,
    )
```

profile of v0, /device:TPU:0, one launch (start us, length us, event | category | flops | bytes accessed | tf_op | source)
XLA Modules:
  0.0 81.1 jit_solution(3935069047673425926)
XLA Ops:
  6.5 0.7 all-gather.4.cloned.1.call-update
  7.3 2.2 %all_gather.16 = bf16[1024,16]{0,1:T(8,128)(2,1)S(1)} all-gather(bf16[512,16]{0,1:T(8,128)(2,1)} %param.15), channel_id=1, replica_groups=mesh['lat'=16,'lon'=2] {'lon'}, dimensions={0}, use_global_device_ids=true | all-gather | bytes 49152 | tf_op jit(solution)/shard_map/all_gather | solution.py:65
  9.5 0.7 exponential_negate_fusion
  10.2 0.9 %compare_select_fusion = f32[128,16]{0,1:T(8,128)S(1)} fusion(bf16[1024,16]{0,1:T(8,128)(2,1)S(1)} %all_gather.16, bf16[128,1,1024]{2,0,1:T(8,128)(2,1)S(1)} %copy-done, f32[16]{0:T(128)} %param.18), kind=kOutput, calls=%fused_computation.69 | convolution fusion | flops 4212736 | bytes 303168 | tf_op jit(solution)/shard_map/dot_general | solution.py:69
  11.0 0.1 multiply_bitcast_fusion
  11.1 0.1 copy.21
  11.2 0.1 fusion.47
  11.3 2.9 %collective-permute-start.2 = (f32[1,16]{1,0:T(1,128)S(1)}, f32[1,16]{1,0:T(1,128)S(1)}, u32[]{:S(2)}, u32[]{:S(2)}) collective-permute-start(f32[1,16]{1,0:T(1,128)S(1)} %get-tuple-element.11), channel_id=1, source_target_pairs={{0,2},{2,0},{4,6},{6,4},{8,10},{10,8},{12,14},{14,12},{16,18},{18,... | collective-permute-start | bytes 200 | tf_op jit(solution)/shard_map/ppermute | solution.py:23
  14.2 2.2 %all_gather.17 = bf16[1024,128]{1,0:T(8,128)(2,1)S(1)} all-gather(bf16[512,128]{1,0:T(8,128)(2,1)} %param.14), channel_id=1, replica_groups=mesh['lat'=16,'lon'=2] {'lon'}, dimensions={0}, use_global_device_ids=true | all-gather | bytes 393216 | tf_op jit(solution)/shard_map/all_gather | solution.py:64
  16.4 0.2 convolution_convert_fusion.3
  16.7 1.9 %collective-permute-start.1 = (bf16[3,1,128]{2,0,1:T(4,128)(2,1)S(1)}, bf16[3,1,128]{2,0,1:T(4,128)(2,1)S(1)}, u32[]{:S(2)}, u32[]{:S(2)}) collective-permute-start(bf16[3,1,128]{2,0,1:T(4,128)(2,1)S(1)} %slice_bitcast_fusion.3), channel_id=1, source_target_pairs={{0,2},{2,4},{4,6},{6,8},{8,10},{10,12},{12,14},{14,16},{16,18},{18... | collective-permute-start | bytes 2312 | tf_op jit(solution)/shard_map/ppermute | solution.py:13
  18.6 0.0 all-gather.8.cloned.1.call-start
  18.7 0.1 copy.22
  18.8 0.1 bitcast_exponential_fusion
  18.9 2.1 %collective-permute-start.3 = (f32[1,16]{1,0:T(1,128)S(1)}, f32[1,16]{1,0:T(1,128)S(1)}, u32[]{:S(2)}, u32[]{:S(2)}) collective-permute-start(f32[1,16]{1,0:T(1,128)S(1)} %get-tuple-element.10), channel_id=1, source_target_pairs={{0,4},{4,0},{2,6},{6,2},{8,12},{12,8},{10,14},{14,10},{16,20},{20,... | collective-permute-start | bytes 200 | tf_op jit(solution)/shard_map/ppermute | solution.py:23
  21.1 0.1 multiply_convert_fusion.3
  21.1 1.1 %all-gather.4.cloned.1.call-done = bf16[1024,1024]{1,0:T(8,128)(2,1)} async-done(((bf16[512,1024]{1,0:T(8,128)(2,1)}), bf16[1024,1024]{1,0:T(8,128)(2,1)}) %all-gather.4.cloned.1.call-update) | async-done | bytes 2097168 | tf_op jit(solution)/shard_map/all_gather | solution.py:62
  22.2 2.0 %convolution_convert_fusion.2 = bf16[128,1024]{1,0:T(8,128)(2,1)S(1)} fusion(bf16[1024,1024]{1,0:T(8,128)(2,1)} %all-gather.4.cloned.1.call-done, bf16[128,1,1024]{2,0,1:T(8,128)(2,1)S(1)} %copy-done), kind=kOutput, calls=%fused_computation.7 | convolution fusion | flops 268566528 | bytes 2621440 | tf_op jit(solution)/shard_map/dot_general | solution.py:69
  24.3 3.6 %collective-permute-start = (bf16[3,1,1024]{2,0,1:T(4,128)(2,1)S(1)}, bf16[3,1,1024]{2,0,1:T(4,128)(2,1)S(1)}, u32[]{:S(2)}, u32[]{:S(2)}) collective-permute-start(bf16[3,1,1024]{2,0,1:T(4,128)(2,1)S(1)} %slice_bitcast_fusion.2), channel_id=1, source_target_pairs={{0,2},{2,4},{4,6},{6,8},{8,10},{10,12},{12,14},{14,16},{16,18},{18... | collective-permute-start | bytes 18440 | tf_op jit(solution)/shard_map/ppermute | solution.py:13
  27.9 0.1 copy.24
  28.0 1.3 %collective-permute-done = bf16[3,1,1024]{2,0,1:T(4,128)(2,1)S(1)} collective-permute-done((bf16[3,1,1024]{2,0,1:T(4,128)(2,1)S(1)}, bf16[3,1,1024]{2,0,1:T(4,128)(2,1)S(1)}, u32[]{:S(2)}, u32[]{:S(2)}) %collective-permute-start) | collective-permute-done | bytes 6176 | tf_op jit(solution)/shard_map/ppermute | solution.py:13
  29.3 0.1 maximum_convert_fusion
  29.3 0.3 multiply_convert_fusion.1
  29.7 0.2 copy.20
  29.9 0.5 fusion.14
  30.4 0.2 reshape.305
  30.6 2.3 %collective-permute-start.5 = (f32[1,16,4096]{2,1,0:T(8,128)S(1)}, f32[1,16,4096]{2,1,0:T(8,128)S(1)}, u32[]{:S(2)}, u32[]{:S(2)}) collective-permute-start(f32[1,16,4096]{2,1,0:T(8,128)S(1)} %reshape.305), channel_id=1, source_target_pairs={{0,2},{2,0},{4,6},{6,4},{8,10},{10,8},{12,14},{14,12},{16,18},{18,... | collective-permute-start | bytes 786440 | tf_op jit(solution)/shard_map/ppermute | solution.py:23
  32.9 3.6 %collective-permute-start.4 = (f32[1,16]{1,0:T(1,128)S(1)}, f32[1,16]{1,0:T(1,128)S(1)}, u32[]{:S(2)}, u32[]{:S(2)}) collective-permute-start(f32[1,16]{1,0:T(1,128)S(1)} %get-tuple-element.8), channel_id=1, source_target_pairs={{0,8},{8,0},{2,10},{10,2},{4,12},{12,4},{6,14},{14,6},{16,24},{24,... | collective-permute-start | bytes 200 | tf_op jit(solution)/shard_map/ppermute | solution.py:23
  36.5 1.5 %collective-permute-done.4 = f32[1,16]{1,0:T(1,128)S(1)} collective-permute-done((f32[1,16]{1,0:T(1,128)S(1)}, f32[1,16]{1,0:T(1,128)S(1)}, u32[]{:S(2)}, u32[]{:S(2)}) %collective-permute-start.4) | collective-permute-done | bytes 96 | tf_op jit(solution)/shard_map/ppermute | solution.py:23
  38.1 0.5 collective-permute-done.5
  38.5 0.1 add_select_fusion.5
  38.7 2.7 %collective-permute-start.6 = (f32[1,16,4096]{2,1,0:T(8,128)S(1)}, f32[1,16,4096]{2,1,0:T(8,128)S(1)}, u32[]{:S(2)}, u32[]{:S(2)}) collective-permute-start(f32[1,16,4096]{2,1,0:T(8,128)S(1)} %add_select_fusion.5), channel_id=1, source_target_pairs={{0,4},{4,0},{2,6},{6,2},{8,12},{12,8},{10,14},{14,10},{16,20},{20,... | collective-permute-start | bytes 786440 | tf_op jit(solution)/shard_map/ppermute | solution.py:23
  41.4 4.4 %collective-permute-done.6 = f32[1,16,4096]{2,1,0:T(8,128)S(1)} collective-permute-done((f32[1,16,4096]{2,1,0:T(8,128)S(1)}, f32[1,16,4096]{2,1,0:T(8,128)S(1)}, u32[]{:S(2)}, u32[]{:S(2)}) %collective-permute-start.6) | collective-permute-done | bytes 262176 | tf_op jit(solution)/shard_map/ppermute | solution.py:23
  45.7 0.1 add_select_fusion.4
  45.9 3.7 %collective-permute-start.7 = (f32[1,16,4096]{2,1,0:T(8,128)S(1)}, f32[1,16,4096]{2,1,0:T(8,128)S(1)}, u32[]{:S(2)}, u32[]{:S(2)}) collective-permute-start(f32[1,16,4096]{2,1,0:T(8,128)S(1)} %add_select_fusion.4), channel_id=1, source_target_pairs={{0,8},{8,0},{2,10},{10,2},{4,12},{12,4},{6,14},{14,6},{16,24},{24,... | collective-permute-start | bytes 786440 | tf_op jit(solution)/shard_map/ppermute | solution.py:23
  49.6 6.6 %collective-permute-done.7 = f32[1,16,4096]{2,1,0:T(8,128)S(1)} collective-permute-done((f32[1,16,4096]{2,1,0:T(8,128)S(1)}, f32[1,16,4096]{2,1,0:T(8,128)S(1)}, u32[]{:S(2)}, u32[]{:S(2)}) %collective-permute-start.7) | collective-permute-done | bytes 262176 | tf_op jit(solution)/shard_map/ppermute | solution.py:23
  56.2 0.1 add_select_fusion.3
  56.4 3.4 %collective-permute-start.8 = (f32[1,16,4096]{2,1,0:T(8,128)S(1)}, f32[1,16,4096]{2,1,0:T(8,128)S(1)}, u32[]{:S(2)}, u32[]{:S(2)}) collective-permute-start(f32[1,16,4096]{2,1,0:T(8,128)S(1)} %add_select_fusion.3), channel_id=1, source_target_pairs={{0,16},{16,0},{2,18},{18,2},{4,20},{20,4},{6,22},{22,6},{8,24},{24... | collective-permute-start | bytes 786440 | tf_op jit(solution)/shard_map/ppermute | solution.py:23
  59.8 0.2 convolution_bitcast_fusion.2
  60.0 0.1 copy.23
  60.1 6.8 %collective-permute-done.8 = f32[1,16,4096]{2,1,0:T(8,128)S(1)} collective-permute-done((f32[1,16,4096]{2,1,0:T(8,128)S(1)}, f32[1,16,4096]{2,1,0:T(8,128)S(1)}, u32[]{:S(2)}, u32[]{:S(2)}) %collective-permute-start.8) | collective-permute-done | bytes 262176 | tf_op jit(solution)/shard_map/ppermute | solution.py:23
  66.9 0.2 add_select_fusion
  67.1 0.2 reshape.306
  67.3 0.6 fusion.1
  68.0 1.3 %fusion = f32[128,1,16,64]{0,3,2,1:T(8,128)S(1)} fusion(f32[128,1,16,64]{0,3,2,1:T(8,128)S(1)} %fusion.1, bf16[128,16,64]{0,2,1:T(8,128)(2,1)S(1)} %bitcast.106, f32[128,16]{0,1:T(8,128)S(1)} %compare_select_fusion, f32[128,128]{1,0:T(8,128)S(1)} %copy.23, f32[128,16]{0,1:T(8,128)S(1)} %bitcast.109, pred[128,128]{1,0:T(8,128)(4,1)S(1)} %iota_compare_fusion), kind=kOutput, calls=%fused_computation.2 | convolution fusion | flops 202506240 | bytes 1409024 | tf_op jit(solution)/shard_map/tsch,schp->tchp/dot_general | solution.py:91
  69.3 0.2 copy.27
  69.5 2.2 %multiply_reduce_fusion = (f32[128]{0:T(128)S(1)}, f32[128,1024]{1,0:T(8,128)S(1)}) fusion(f32[128,1024]{1,0:T(8,128)S(1)} %copy.27, bf16[1024,1024]{1,0:T(8,128)(2,1)} %all-gather.6.cloned.1.call-done, bf16[128,1,1024]{2,0,1:T(8,128)(2,1)S(1)} %copy-done), kind=kOutput, calls=%fused_computation.27 | convolution fusion | flops 269614976 | bytes 3408384 | tf_op jit(solution)/shard_map/dot_general | solution.py:69
  71.7 2.8 %fusion.3 = bf16[128,1,1024]{2,0,1:T(8,128)(2,1)} fusion(bf16[1024,1024]{1,0:T(8,128)(2,1)} %all-gather.8.cloned.1.call-done, f32[128,1024]{1,0:T(8,128)S(1)} %get-tuple-element.28, f32[1024]{0:T(1024)S(1)} %copy-done.2, f32[128]{0:T(128)S(1)} %add_rsqrt_fusion), kind=kOutput, calls=%fused_computation.8 | convolution fusion | flops 268959744 | bytes 2888192 | tf_op jit(solution)/shard_map/dot_general | solution.py:128
  (31 shorter events, 0.3 us)
Async XLA Ops:
  6.5 3.6 %copy-start = (bf16[128,1,1024]{2,0,1:T(8,128)(2,1)S(1)}, bf16[128,1,1024]{2,0,1:T(8,128)(2,1)}, u32[]{:S(2)}) copy-start(bf16[128,1,1024]{2,0,1:T(8,128)(2,1)} %param.11) | copy-start | bytes 786436
  6.5 12.2 %copy-start.3 = (f32[4,128]{1,0:T(4,128)S(1)}, f32[4,128]{1,0:T(4,128)}, u32[]{:S(2)}) copy-start(f32[4,128]{1,0:T(4,128)} %param.17) | copy-start | bytes 6148
  6.5 12.3 %copy-start.1 = (f32[4,1024]{1,0:T(4,128)S(1)}, f32[4,1024]{1,0:T(4,128)}, u32[]{:S(2)}) copy-start(f32[4,1024]{1,0:T(4,128)} %param.16) | copy-start | bytes 49156
  6.5 15.7 %all-gather.4.cloned.1.call-start = ((), (), s32[]{:S(2)}) async-start(), calls=%async_computation | async-start | bytes 3145728 | tf_op jit(solution)/shard_map/all_gather | solution.py:62
  7.3 62.2 %all-gather.6.cloned.1.call-start = ((), (), s32[]{:S(2)}) async-start(), calls=%async_computation.1 | async-start | bytes 3145728 | tf_op jit(solution)/shard_map/all_gather | solution.py:63
  11.3 7.6 %collective-permute-start.2 = (f32[1,16]{1,0:T(1,128)S(1)}, f32[1,16]{1,0:T(1,128)S(1)}, u32[]{:S(2)}, u32[]{:S(2)}) collective-permute-start(f32[1,16]{1,0:T(1,128)S(1)} %get-tuple-element.11), channel_id=1, source_target_pairs={{0,2},{2,0},{4,6},{6,4},{8,10},{10,8},{12,14},{14,12},{16,18},{18,... | collective-permute-start | bytes 200 | tf_op jit(solution)/shard_map/ppermute | solution.py:23
  16.7 4.4 %collective-permute-start.1 = (bf16[3,1,128]{2,0,1:T(4,128)(2,1)S(1)}, bf16[3,1,128]{2,0,1:T(4,128)(2,1)S(1)}, u32[]{:S(2)}, u32[]{:S(2)}) collective-permute-start(bf16[3,1,128]{2,0,1:T(4,128)(2,1)S(1)} %slice_bitcast_fusion.3), channel_id=1, source_target_pairs={{0,2},{2,4},{4,6},{6,8},{8,10},{10,12},{12,14},{14,16},{16,18},{18... | collective-permute-start | bytes 2312 | tf_op jit(solution)/shard_map/ppermute | solution.py:13
  18.6 53.1 %all-gather.8.cloned.1.call-start = ((), (), s32[]{:S(2)}) async-start(), calls=%async_computation.2 | async-start | bytes 3145728 | tf_op jit(solution)/shard_map/all_gather | solution.py:130
  18.9 14.0 %collective-permute-start.3 = (f32[1,16]{1,0:T(1,128)S(1)}, f32[1,16]{1,0:T(1,128)S(1)}, u32[]{:S(2)}, u32[]{:S(2)}) collective-permute-start(f32[1,16]{1,0:T(1,128)S(1)} %get-tuple-element.10), channel_id=1, source_target_pairs={{0,4},{4,0},{2,6},{6,2},{8,12},{12,8},{10,14},{14,10},{16,20},{20,... | collective-permute-start | bytes 200 | tf_op jit(solution)/shard_map/ppermute | solution.py:23
  24.3 5.0 %collective-permute-start = (bf16[3,1,1024]{2,0,1:T(4,128)(2,1)S(1)}, bf16[3,1,1024]{2,0,1:T(4,128)(2,1)S(1)}, u32[]{:S(2)}, u32[]{:S(2)}) collective-permute-start(bf16[3,1,1024]{2,0,1:T(4,128)(2,1)S(1)} %slice_bitcast_fusion.2), channel_id=1, source_target_pairs={{0,2},{2,4},{4,6},{6,8},{8,10},{10,12},{12,14},{14,16},{16,18},{18... | collective-permute-start | bytes 18440 | tf_op jit(solution)/shard_map/ppermute | solution.py:13
  30.6 8.0 %collective-permute-start.5 = (f32[1,16,4096]{2,1,0:T(8,128)S(1)}, f32[1,16,4096]{2,1,0:T(8,128)S(1)}, u32[]{:S(2)}, u32[]{:S(2)}) collective-permute-start(f32[1,16,4096]{2,1,0:T(8,128)S(1)} %reshape.305), channel_id=1, source_target_pairs={{0,2},{2,0},{4,6},{6,4},{8,10},{10,8},{12,14},{14,12},{16,18},{18,... | collective-permute-start | bytes 786440 | tf_op jit(solution)/shard_map/ppermute | solution.py:23
  32.9 5.1 %collective-permute-start.4 = (f32[1,16]{1,0:T(1,128)S(1)}, f32[1,16]{1,0:T(1,128)S(1)}, u32[]{:S(2)}, u32[]{:S(2)}) collective-permute-start(f32[1,16]{1,0:T(1,128)S(1)} %get-tuple-element.8), channel_id=1, source_target_pairs={{0,8},{8,0},{2,10},{10,2},{4,12},{12,4},{6,14},{14,6},{16,24},{24,... | collective-permute-start | bytes 200 | tf_op jit(solution)/shard_map/ppermute | solution.py:23
  38.7 7.1 %collective-permute-start.6 = (f32[1,16,4096]{2,1,0:T(8,128)S(1)}, f32[1,16,4096]{2,1,0:T(8,128)S(1)}, u32[]{:S(2)}, u32[]{:S(2)}) collective-permute-start(f32[1,16,4096]{2,1,0:T(8,128)S(1)} %add_select_fusion.5), channel_id=1, source_target_pairs={{0,4},{4,0},{2,6},{6,2},{8,12},{12,8},{10,14},{14,10},{16,20},{20,... | collective-permute-start | bytes 786440 | tf_op jit(solution)/shard_map/ppermute | solution.py:23
  45.9 10.4 %collective-permute-start.7 = (f32[1,16,4096]{2,1,0:T(8,128)S(1)}, f32[1,16,4096]{2,1,0:T(8,128)S(1)}, u32[]{:S(2)}, u32[]{:S(2)}) collective-permute-start(f32[1,16,4096]{2,1,0:T(8,128)S(1)} %add_select_fusion.4), channel_id=1, source_target_pairs={{0,8},{8,0},{2,10},{10,2},{4,12},{12,4},{6,14},{14,6},{16,24},{24,... | collective-permute-start | bytes 786440 | tf_op jit(solution)/shard_map/ppermute | solution.py:23
  56.4 10.6 %collective-permute-start.8 = (f32[1,16,4096]{2,1,0:T(8,128)S(1)}, f32[1,16,4096]{2,1,0:T(8,128)S(1)}, u32[]{:S(2)}, u32[]{:S(2)}) collective-permute-start(f32[1,16,4096]{2,1,0:T(8,128)S(1)} %add_select_fusion.3), channel_id=1, source_target_pairs={{0,16},{16,0},{2,18},{18,2},{4,20},{20,4},{6,22},{22,6},{8,24},{24... | collective-permute-start | bytes 786440 | tf_op jit(solution)/shard_map/ppermute | solution.py:23
  69.5 2.3 %copy-start.2 = (f32[1024]{0:T(1024)S(1)}, f32[1024]{0:T(1024)}, u32[]{:S(2)}) copy-start(f32[1024]{0:T(1024)} %param.20) | copy-start | bytes 12292
Sparse Core Ops, SparseCore 0:
  8.9 13.2 all-gather.3
  23.8 11.7 all-gather.5
  49.7 8.9 all-gather.7
where the time goes:
time: 81.4 us; the launch traced here: 81.1 us
  starting transfers between devices  26.3 us (32%)
  waiting for transfers between devices  23 us (28%)
  between operations  13.4 us (16%)
  matrix products  10.8 us (13%)
  blocking collectives  4.38 us (5%)
  other arithmetic  1.99 us (2%)
  local copies, waits for them, and re-layouts  1.17 us (1%)
    ppermute x7, starting transfers between devices, partner_2(): return lax.ppermute(block, axis, route)  20.7 us
    ppermute x7, waiting for transfers between devices, partner_2(): return lax.ppermute(block, axis, route)  19.9 us
    ppermute x2, starting transfers between devices, shifted(): return lax.ppermute(block, axis, route)  5.56 us
    dot_general x4, matrix products, local(): jnp.dot(columns, piece_rows, preferred_element_type=jnp.float32)  5.28 us
    dot_general x1, matrix products, local(): jnp.dot(columns, lax.all_gather(proj_out, 'lon', axis=0, tiled=True), pre...  2.81 us
    all_gather x1, blocking collectives, local(): lax.all_gather(proj_bc, 'lon', axis=0, tiled=True)  2.19 us
    all_gather x1, blocking collectives, local(): lax.all_gather(proj_dt, 'lon', axis=0, tiled=True)  2.19 us
  transfers between devices with their start and end apart: 12, of which 7 were waited for; matrix products, arithmetic and copies ran while one was open for 14% of the time, Pallas kernels for 0%

commit v1 on v0

--- a/solution.py
+++ b/solution.py
@@ -62,7 +62,9 @@
         lax.all_gather(proj_x, "lon", axis=0, tiled=True),
         lax.all_gather(proj_z, "lon", axis=0, tiled=True),
         lax.all_gather(proj_bc, "lon", axis=0, tiled=True),
-        lax.all_gather(proj_dt, "lon", axis=0, tiled=True),
+        jnp.concatenate(
+            lax.all_to_all(jnp.stack([proj_dt] * lax.axis_size("lon")), "lon", 0, 0), axis=0
+        ),
     )
     columns = flat_rows
     projected = tuple(

time: 81.4 us -> 83.9 us (1.031)
  starting transfers between devices: 26.3 us -> 28 us
  blocking collectives: 4.38 us -> 5.93 us
  waiting for transfers between devices: 23 us -> 21.5 us
    all_to_all x0 -> x1, blocking collectives: none -> 3.73 us  [local(): lax.all_to_all(jnp.stack([proj_dt] * lax.axis_size('lon')), 'lon', 0, 0)]
    all_gather x1 -> x0, blocking collectives: 2.19 us -> none  [local(): lax.all_gather(proj_dt, 'lon', axis=0, tiled=True)]
    all_gather x1, waiting for transfers between devices: 1.1 us -> 0.02 us  [local(): lax.all_gather(proj_x, 'lon', axis=0, tiled=True)]
    ppermute x7, starting transfers between devices: 20.7 us -> 21.6 us  [partner_2(): return lax.ppermute(block, axis, route)]
  transfers between devices with their start and end apart: 12 -> 12, of which waited for: 7 -> 5; matrix products, arithmetic and copies ran while one was open for 14% -> 14% of each run, Pallas kernels for 0% -> 0%
where the time goes in v1:
time: 83.9 us; the launch traced here: 83.6 us
  starting transfers between devices  28 us (33%)
  waiting for transfers between devices  21.5 us (26%)
  between operations  13.5 us (16%)
  matrix products  10.8 us (13%)
  blocking collectives  5.93 us (7%)
  other arithmetic  2.79 us (3%)
  local copies, waits for them, and re-layouts  1.17 us (1%)
    ppermute x7, starting transfers between devices, partner_2(): return lax.ppermute(block, axis, route)  21.6 us
    ppermute x7, waiting for transfers between devices, partner_2(): return lax.ppermute(block, axis, route)  19.4 us
    ppermute x2, starting transfers between devices, shifted(): return lax.ppermute(block, axis, route)  6.28 us
    dot_general x4, matrix products, local(): jnp.dot(columns, piece_rows, preferred_element_type=jnp.float32)  5.29 us
    all_to_all x1, blocking collectives, local(): lax.all_to_all(jnp.stack([proj_dt] * lax.axis_size('lon')), 'lon', 0, 0)  3.73 us
    dot_general x1, matrix products, local(): jnp.dot(columns, lax.all_gather(proj_out, 'lon', axis=0, tiled=True), pre...  2.81 us
    all_gather x1, blocking collectives, local(): lax.all_gather(proj_bc, 'lon', axis=0, tiled=True)  2.19 us
  transfers between devices with their start and end apart: 12, of which 5 were waited for; matrix products, arithmetic and copies ran while one was open for 14% of the time, Pallas kernels for 0%

profile of v1, /device:TPU:0, one launch (start us, length us, event | category | flops | bytes accessed | tf_op | source)
XLA Modules:
  0.0 83.6 jit_solution(12960277766635121128)
XLA Ops:
  6.5 0.7 all-gather.4.cloned.1.call-update
  7.3 0.0 all-gather.6.cloned.1.call-start
  7.3 0.8 pad_maximum_fusion
  8.1 3.7 %all_to_all.5 = bf16[2,512,16]{1,2,0:T(8,128)(2,1)S(1)} all-to-all(bf16[2,512,16]{1,2,0:T(8,128)(2,1)S(1)} %pad_maximum_fusion), channel_id=1, replica_groups=mesh['lat'=16,'lon'=2] {'lon'}, dimensions={0} | all-to-all | bytes 65536 | tf_op jit(solution)/shard_map/all_to_all | solution.py:66
  11.8 0.7 exponential_negate_fusion
  12.5 0.9 %compare_select_fusion = f32[128,16]{0,1:T(8,128)S(1)} fusion(bf16[1024,16]{0,1:T(8,128)(2,1)S(1)} %bitcast.117, bf16[128,1,1024]{2,0,1:T(8,128)(2,1)S(1)} %copy-done, f32[16]{0:T(128)} %param.18), kind=kOutput, calls=%fused_computation.71 | convolution fusion | flops 4212736 | bytes 303168 | tf_op jit(solution)/shard_map/dot_general | solution.py:71
  13.4 0.1 multiply_bitcast_fusion
  13.4 0.1 copy.22
  13.6 0.1 fusion.48
  13.7 3.0 %collective-permute-start.2 = (f32[1,16]{1,0:T(1,128)S(1)}, f32[1,16]{1,0:T(1,128)S(1)}, u32[]{:S(2)}, u32[]{:S(2)}) collective-permute-start(f32[1,16]{1,0:T(1,128)S(1)} %get-tuple-element.11), channel_id=1, source_target_pairs={{0,2},{2,0},{4,6},{6,4},{8,10},{10,8},{12,14},{14,12},{16,18},{18,... | collective-permute-start | bytes 200 | tf_op jit(solution)/shard_map/ppermute | solution.py:23
  16.7 2.2 %all_gather.13 = bf16[1024,128]{1,0:T(8,128)(2,1)S(1)} all-gather(bf16[512,128]{1,0:T(8,128)(2,1)} %param.14), channel_id=1, replica_groups=mesh['lat'=16,'lon'=2] {'lon'}, dimensions={0}, use_global_device_ids=true | all-gather | bytes 393216 | tf_op jit(solution)/shard_map/all_gather | solution.py:64
  18.9 0.2 convolution_convert_fusion.3
  19.2 1.9 %collective-permute-start.1 = (bf16[3,1,128]{2,0,1:T(4,128)(2,1)S(1)}, bf16[3,1,128]{2,0,1:T(4,128)(2,1)S(1)}, u32[]{:S(2)}, u32[]{:S(2)}) collective-permute-start(bf16[3,1,128]{2,0,1:T(4,128)(2,1)S(1)} %slice_bitcast_fusion.3), channel_id=1, source_target_pairs={{0,2},{2,4},{4,6},{6,8},{8,10},{10,12},{12,14},{14,16},{16,18},{18... | collective-permute-start | bytes 2312 | tf_op jit(solution)/shard_map/ppermute | solution.py:13
  21.1 0.0 all-gather.8.cloned.1.call-start
  21.2 0.1 copy.23
  21.3 0.1 bitcast_exponential_fusion
  21.4 2.1 %collective-permute-start.3 = (f32[1,16]{1,0:T(1,128)S(1)}, f32[1,16]{1,0:T(1,128)S(1)}, u32[]{:S(2)}, u32[]{:S(2)}) collective-permute-start(f32[1,16]{1,0:T(1,128)S(1)} %get-tuple-element.10), channel_id=1, source_target_pairs={{0,4},{4,0},{2,6},{6,2},{8,12},{12,8},{10,14},{14,10},{16,20},{20,... | collective-permute-start | bytes 200 | tf_op jit(solution)/shard_map/ppermute | solution.py:23
  23.6 0.1 multiply_convert_fusion.3
  23.6 2.0 %convolution_convert_fusion.2 = bf16[128,1024]{1,0:T(8,128)(2,1)S(1)} fusion(bf16[1024,1024]{1,0:T(8,128)(2,1)} %all-gather.4.cloned.1.call-done, bf16[128,1,1024]{2,0,1:T(8,128)(2,1)S(1)} %copy-done), kind=kOutput, calls=%fused_computation.7 | convolution fusion | flops 268566528 | bytes 2621440 | tf_op jit(solution)/shard_map/dot_general | solution.py:71
  25.7 4.3 %collective-permute-start = (bf16[3,1,1024]{2,0,1:T(4,128)(2,1)S(1)}, bf16[3,1,1024]{2,0,1:T(4,128)(2,1)S(1)}, u32[]{:S(2)}, u32[]{:S(2)}) collective-permute-start(bf16[3,1,1024]{2,0,1:T(4,128)(2,1)S(1)} %slice_bitcast_fusion.2), channel_id=1, source_target_pairs={{0,2},{2,4},{4,6},{6,8},{8,10},{10,12},{12,14},{14,16},{16,18},{18... | collective-permute-start | bytes 18440 | tf_op jit(solution)/shard_map/ppermute | solution.py:13
  30.1 0.1 copy.25
  30.1 1.3 %collective-permute-done = bf16[3,1,1024]{2,0,1:T(4,128)(2,1)S(1)} collective-permute-done((bf16[3,1,1024]{2,0,1:T(4,128)(2,1)S(1)}, bf16[3,1,1024]{2,0,1:T(4,128)(2,1)S(1)}, u32[]{:S(2)}, u32[]{:S(2)}) %collective-permute-start) | collective-permute-done | bytes 6176 | tf_op jit(solution)/shard_map/ppermute | solution.py:13
  31.4 0.1 maximum_convert_fusion
  31.5 0.3 multiply_convert_fusion.1
  31.8 0.2 copy.20
  32.0 0.5 fusion.15
  32.5 0.2 reshape.309
  32.7 2.6 %collective-permute-start.5 = (f32[1,16,4096]{2,1,0:T(8,128)S(1)}, f32[1,16,4096]{2,1,0:T(8,128)S(1)}, u32[]{:S(2)}, u32[]{:S(2)}) collective-permute-start(f32[1,16,4096]{2,1,0:T(8,128)S(1)} %reshape.309), channel_id=1, source_target_pairs={{0,2},{2,0},{4,6},{6,4},{8,10},{10,8},{12,14},{14,12},{16,18},{18,... | collective-permute-start | bytes 786440 | tf_op jit(solution)/shard_map/ppermute | solution.py:23
  35.3 3.7 %collective-permute-start.4 = (f32[1,16]{1,0:T(1,128)S(1)}, f32[1,16]{1,0:T(1,128)S(1)}, u32[]{:S(2)}, u32[]{:S(2)}) collective-permute-start(f32[1,16]{1,0:T(1,128)S(1)} %get-tuple-element.8), channel_id=1, source_target_pairs={{0,8},{8,0},{2,10},{10,2},{4,12},{12,4},{6,14},{14,6},{16,24},{24,... | collective-permute-start | bytes 200 | tf_op jit(solution)/shard_map/ppermute | solution.py:23
  39.0 1.5 %collective-permute-done.4 = f32[1,16]{1,0:T(1,128)S(1)} collective-permute-done((f32[1,16]{1,0:T(1,128)S(1)}, f32[1,16]{1,0:T(1,128)S(1)}, u32[]{:S(2)}, u32[]{:S(2)}) %collective-permute-start.4) | collective-permute-done | bytes 96 | tf_op jit(solution)/shard_map/ppermute | solution.py:23
  40.6 0.1 add_select_fusion.5
  40.7 2.9 %collective-permute-start.6 = (f32[1,16,4096]{2,1,0:T(8,128)S(1)}, f32[1,16,4096]{2,1,0:T(8,128)S(1)}, u32[]{:S(2)}, u32[]{:S(2)}) collective-permute-start(f32[1,16,4096]{2,1,0:T(8,128)S(1)} %add_select_fusion.5), channel_id=1, source_target_pairs={{0,4},{4,0},{2,6},{6,2},{8,12},{12,8},{10,14},{14,10},{16,20},{20,... | collective-permute-start | bytes 786440 | tf_op jit(solution)/shard_map/ppermute | solution.py:23
  43.6 4.4 %collective-permute-done.6 = f32[1,16,4096]{2,1,0:T(8,128)S(1)} collective-permute-done((f32[1,16,4096]{2,1,0:T(8,128)S(1)}, f32[1,16,4096]{2,1,0:T(8,128)S(1)}, u32[]{:S(2)}, u32[]{:S(2)}) %collective-permute-start.6) | collective-permute-done | bytes 262176 | tf_op jit(solution)/shard_map/ppermute | solution.py:23
  47.9 0.1 add_select_fusion.4
  48.1 3.9 %collective-permute-start.7 = (f32[1,16,4096]{2,1,0:T(8,128)S(1)}, f32[1,16,4096]{2,1,0:T(8,128)S(1)}, u32[]{:S(2)}, u32[]{:S(2)}) collective-permute-start(f32[1,16,4096]{2,1,0:T(8,128)S(1)} %add_select_fusion.4), channel_id=1, source_target_pairs={{0,8},{8,0},{2,10},{10,2},{4,12},{12,4},{6,14},{14,6},{16,24},{24,... | collective-permute-start | bytes 786440 | tf_op jit(solution)/shard_map/ppermute | solution.py:23
  52.1 6.6 %collective-permute-done.7 = f32[1,16,4096]{2,1,0:T(8,128)S(1)} collective-permute-done((f32[1,16,4096]{2,1,0:T(8,128)S(1)}, f32[1,16,4096]{2,1,0:T(8,128)S(1)}, u32[]{:S(2)}, u32[]{:S(2)}) %collective-permute-start.7) | collective-permute-done | bytes 262176 | tf_op jit(solution)/shard_map/ppermute | solution.py:23
  58.7 0.1 add_select_fusion.3
  58.9 3.4 %collective-permute-start.8 = (f32[1,16,4096]{2,1,0:T(8,128)S(1)}, f32[1,16,4096]{2,1,0:T(8,128)S(1)}, u32[]{:S(2)}, u32[]{:S(2)}) collective-permute-start(f32[1,16,4096]{2,1,0:T(8,128)S(1)} %add_select_fusion.3), channel_id=1, source_target_pairs={{0,16},{16,0},{2,18},{18,2},{4,20},{20,4},{6,22},{22,6},{8,24},{24... | collective-permute-start | bytes 786440 | tf_op jit(solution)/shard_map/ppermute | solution.py:23
  62.3 0.2 convolution_bitcast_fusion.2
  62.5 0.1 copy.24
  62.6 6.8 %collective-permute-done.8 = f32[1,16,4096]{2,1,0:T(8,128)S(1)} collective-permute-done((f32[1,16,4096]{2,1,0:T(8,128)S(1)}, f32[1,16,4096]{2,1,0:T(8,128)S(1)}, u32[]{:S(2)}, u32[]{:S(2)}) %collective-permute-start.8) | collective-permute-done | bytes 262176 | tf_op jit(solution)/shard_map/ppermute | solution.py:23
  69.4 0.2 add_select_fusion
  69.6 0.2 reshape.310
  69.8 0.6 fusion.1
  70.5 1.3 %fusion = f32[128,1,16,64]{0,3,2,1:T(8,128)S(1)} fusion(f32[128,1,16,64]{0,3,2,1:T(8,128)S(1)} %fusion.1, bf16[128,16,64]{0,2,1:T(8,128)(2,1)S(1)} %bitcast.113, f32[128,16]{0,1:T(8,128)S(1)} %compare_select_fusion, f32[128,128]{1,0:T(8,128)S(1)} %copy.24, f32[128,16]{0,1:T(8,128)S(1)} %bitcast.118, pred[128,128]{1,0:T(8,128)(4,1)S(1)} %iota_compare_fusion), kind=kOutput, calls=%fused_computation.2 | convolution fusion | flops 202506240 | bytes 1409024 | tf_op jit(solution)/shard_map/tsch,schp->tchp/dot_general | solution.py:93
  71.8 0.2 copy.28
  72.0 2.2 %multiply_reduce_fusion = (f32[128]{0:T(128)S(1)}, f32[128,1024]{1,0:T(8,128)S(1)}) fusion(f32[128,1024]{1,0:T(8,128)S(1)} %copy.28, bf16[1024,1024]{1,0:T(8,128)(2,1)} %all-gather.6.cloned.1.call-done, bf16[128,1,1024]{2,0,1:T(8,128)(2,1)S(1)} %copy-done), kind=kOutput, calls=%fused_computation.28 | convolution fusion | flops 269614976 | bytes 3408384 | tf_op jit(solution)/shard_map/dot_general | solution.py:71
  74.2 2.8 %fusion.3 = bf16[128,1,1024]{2,0,1:T(8,128)(2,1)} fusion(bf16[1024,1024]{1,0:T(8,128)(2,1)} %all-gather.8.cloned.1.call-done, f32[128,1024]{1,0:T(8,128)S(1)} %get-tuple-element.28, f32[1024]{0:T(1024)S(1)} %copy-done.2, f32[128]{0:T(128)S(1)} %add_rsqrt_fusion), kind=kOutput, calls=%fused_computation.8 | convolution fusion | flops 268959744 | bytes 2888192 | tf_op jit(solution)/shard_map/dot_general | solution.py:130
  (33 shorter events, 0.2 us)
Async XLA Ops:
  6.5 6.0 %copy-start = (bf16[128,1,1024]{2,0,1:T(8,128)(2,1)S(1)}, bf16[128,1,1024]{2,0,1:T(8,128)(2,1)}, u32[]{:S(2)}) copy-start(bf16[128,1,1024]{2,0,1:T(8,128)(2,1)} %param.11) | copy-start | bytes 786436
  6.5 14.7 %copy-start.3 = (f32[4,128]{1,0:T(4,128)S(1)}, f32[4,128]{1,0:T(4,128)}, u32[]{:S(2)}) copy-start(f32[4,128]{1,0:T(4,128)} %param.17) | copy-start | bytes 6148
  6.5 14.8 %copy-start.1 = (f32[4,1024]{1,0:T(4,128)S(1)}, f32[4,1024]{1,0:T(4,128)}, u32[]{:S(2)}) copy-start(f32[4,1024]{1,0:T(4,128)} %param.16) | copy-start | bytes 49156
  6.5 17.1 %all-gather.4.cloned.1.call-start = ((), (), s32[]{:S(2)}) async-start(), calls=%async_computation.1 | async-start | bytes 3145728 | tf_op jit(solution)/shard_map/all_gather | solution.py:62
  7.3 64.7 %all-gather.6.cloned.1.call-start = ((), (), s32[]{:S(2)}) async-start(), calls=%async_computation.2 | async-start | bytes 3145728 | tf_op jit(solution)/shard_map/all_gather | solution.py:63
  13.7 7.7 %collective-permute-start.2 = (f32[1,16]{1,0:T(1,128)S(1)}, f32[1,16]{1,0:T(1,128)S(1)}, u32[]{:S(2)}, u32[]{:S(2)}) collective-permute-start(f32[1,16]{1,0:T(1,128)S(1)} %get-tuple-element.11), channel_id=1, source_target_pairs={{0,2},{2,0},{4,6},{6,4},{8,10},{10,8},{12,14},{14,12},{16,18},{18,... | collective-permute-start | bytes 200 | tf_op jit(solution)/shard_map/ppermute | solution.py:23
  19.2 4.4 %collective-permute-start.1 = (bf16[3,1,128]{2,0,1:T(4,128)(2,1)S(1)}, bf16[3,1,128]{2,0,1:T(4,128)(2,1)S(1)}, u32[]{:S(2)}, u32[]{:S(2)}) collective-permute-start(bf16[3,1,128]{2,0,1:T(4,128)(2,1)S(1)} %slice_bitcast_fusion.3), channel_id=1, source_target_pairs={{0,2},{2,4},{4,6},{6,8},{8,10},{10,12},{12,14},{14,16},{16,18},{18... | collective-permute-start | bytes 2312 | tf_op jit(solution)/shard_map/ppermute | solution.py:13
  21.1 53.1 %all-gather.8.cloned.1.call-start = ((), (), s32[]{:S(2)}) async-start(), calls=%async_computation.3 | async-start | bytes 3145728 | tf_op jit(solution)/shard_map/all_gather | solution.py:132
  21.4 13.9 %collective-permute-start.3 = (f32[1,16]{1,0:T(1,128)S(1)}, f32[1,16]{1,0:T(1,128)S(1)}, u32[]{:S(2)}, u32[]{:S(2)}) collective-permute-start(f32[1,16]{1,0:T(1,128)S(1)} %get-tuple-element.10), channel_id=1, source_target_pairs={{0,4},{4,0},{2,6},{6,2},{8,12},{12,8},{10,14},{14,10},{16,20},{20,... | collective-permute-start | bytes 200 | tf_op jit(solution)/shard_map/ppermute | solution.py:23
  25.7 5.7 %collective-permute-start = (bf16[3,1,1024]{2,0,1:T(4,128)(2,1)S(1)}, bf16[3,1,1024]{2,0,1:T(4,128)(2,1)S(1)}, u32[]{:S(2)}, u32[]{:S(2)}) collective-permute-start(bf16[3,1,1024]{2,0,1:T(4,128)(2,1)S(1)} %slice_bitcast_fusion.2), channel_id=1, source_target_pairs={{0,2},{2,4},{4,6},{6,8},{8,10},{10,12},{12,14},{14,16},{16,18},{18... | collective-permute-start | bytes 18440 | tf_op jit(solution)/shard_map/ppermute | solution.py:13
  32.7 7.8 %collective-permute-start.5 = (f32[1,16,4096]{2,1,0:T(8,128)S(1)}, f32[1,16,4096]{2,1,0:T(8,128)S(1)}, u32[]{:S(2)}, u32[]{:S(2)}) collective-permute-start(f32[1,16,4096]{2,1,0:T(8,128)S(1)} %reshape.309), channel_id=1, source_target_pairs={{0,2},{2,0},{4,6},{6,4},{8,10},{10,8},{12,14},{14,12},{16,18},{18,... | collective-permute-start | bytes 786440 | tf_op jit(solution)/shard_map/ppermute | solution.py:23
  35.3 5.2 %collective-permute-start.4 = (f32[1,16]{1,0:T(1,128)S(1)}, f32[1,16]{1,0:T(1,128)S(1)}, u32[]{:S(2)}, u32[]{:S(2)}) collective-permute-start(f32[1,16]{1,0:T(1,128)S(1)} %get-tuple-element.8), channel_id=1, source_target_pairs={{0,8},{8,0},{2,10},{10,2},{4,12},{12,4},{6,14},{14,6},{16,24},{24,... | collective-permute-start | bytes 200 | tf_op jit(solution)/shard_map/ppermute | solution.py:23
  40.7 7.3 %collective-permute-start.6 = (f32[1,16,4096]{2,1,0:T(8,128)S(1)}, f32[1,16,4096]{2,1,0:T(8,128)S(1)}, u32[]{:S(2)}, u32[]{:S(2)}) collective-permute-start(f32[1,16,4096]{2,1,0:T(8,128)S(1)} %add_select_fusion.5), channel_id=1, source_target_pairs={{0,4},{4,0},{2,6},{6,2},{8,12},{12,8},{10,14},{14,10},{16,20},{20,... | collective-permute-start | bytes 786440 | tf_op jit(solution)/shard_map/ppermute | solution.py:23
  48.1 10.7 %collective-permute-start.7 = (f32[1,16,4096]{2,1,0:T(8,128)S(1)}, f32[1,16,4096]{2,1,0:T(8,128)S(1)}, u32[]{:S(2)}, u32[]{:S(2)}) collective-permute-start(f32[1,16,4096]{2,1,0:T(8,128)S(1)} %add_select_fusion.4), channel_id=1, source_target_pairs={{0,8},{8,0},{2,10},{10,2},{4,12},{12,4},{6,14},{14,6},{16,24},{24,... | collective-permute-start | bytes 786440 | tf_op jit(solution)/shard_map/ppermute | solution.py:23
  58.9 10.6 %collective-permute-start.8 = (f32[1,16,4096]{2,1,0:T(8,128)S(1)}, f32[1,16,4096]{2,1,0:T(8,128)S(1)}, u32[]{:S(2)}, u32[]{:S(2)}) collective-permute-start(f32[1,16,4096]{2,1,0:T(8,128)S(1)} %add_select_fusion.3), channel_id=1, source_target_pairs={{0,16},{16,0},{2,18},{18,2},{4,20},{20,4},{6,22},{22,6},{8,24},{24... | collective-permute-start | bytes 786440 | tf_op jit(solution)/shard_map/ppermute | solution.py:23
  72.0 2.3 %copy-start.2 = (f32[1024]{0:T(1024)S(1)}, f32[1024]{0:T(1024)}, u32[]{:S(2)}) copy-start(f32[1024]{0:T(1024)} %param.20) | copy-start | bytes 12292
Sparse Core Ops, SparseCore 0:
  8.9 13.2 all-gather.3
  23.8 11.7 all-gather.5
  52.2 8.9 all-gather.7
